TPU v7x, 128 devices: a whole 4x4x4 slice. The times are simulated.
128 devices in a mesh: seq: 64 (over x, z_lo, y, core), blk: 2 (over z_hi).
Axes of the slice: x: 4, y: 4, z: 4 (z_hi: 2, z_lo: 2; z = z_hi * 2 + z_lo), core: 2. Of those that a mesh axis runs over, the one named last changes fastest.
Arguments:
- query: bfloat16 [8192, 5120], P(('blk', 'seq')), may hold values from -139 to 139
- keys: bfloat16 [8192, 5120], P(('blk', 'seq')), may hold values from -4.5 to 4.5
- values: bfloat16 [8192, 5120], P(('blk', 'seq')), may hold values from -6 to 6
Outputs:
- attended: bfloat16 [8192, 5120], P(('blk', 'seq'))
All inputs are finite; a program needn't handle non-finite values.
Results may differ from a plain program's by a relative error of at most 0.008.
Values may be sent and summed in bfloat16 or wider, within the bound.
A program may use at most 64 MiB of HBM per device.

v0:
```python
import jax
import jax.numpy as jnp
from jax import lax
from jax.sharding import PartitionSpec as P

HEADS = 40


def partner(value, axis, bit):
    mask = 2**bit
    pairs = [(source, source ^ mask) for source in range(lax.axis_size(axis))]
    return lax.ppermute(value, axis, pairs)


def partial_block(q_rows, k_tile, v_tile):
    scores = lax.dot_general(
        q_rows, k_tile, (((1,), (1,)), ((), ())), preferred_element_type=jnp.float32
    ) * q_rows.shape[1] ** (-0.5)
    peak = jnp.max(scores, axis=1)
    expo = jnp.exp(scores - peak[:, None])
    totals = jnp.sum(expo, axis=1)
    summed = jnp.dot(expo.astype(jnp.bfloat16), v_tile, preferred_element_type=jnp.float32)
    return (peak, totals, summed)


def combine_parts(left, right):
    peak = jnp.maximum(left[0], right[0])
    scale_left = jnp.exp(left[0] - peak)
    scale_right = jnp.exp(right[0] - peak)
    totals = scale_left * left[1] + scale_right * right[1]
    summed = scale_left[:, None] * left[2] + scale_right[:, None] * right[2]
    return (peak, totals, summed)


def attend_rows(q_rows, first_k, first_v, second_k, second_v):
    state = partial_block(q_rows, first_k, first_v)
    state = combine_parts(state, partial_block(q_rows, second_k, second_v))
    return (state[2] / state[1][:, None]).astype(jnp.bfloat16)


def attend_item(args):
    q_head, first_k, first_v, second_k, second_v = args
    length, width = q_head.shape
    rows = min(512, length)

    def block(q_rows):
        return attend_rows(q_rows, first_k, first_v, second_k, second_v)

    return lax.map(block, q_head.reshape(length // rows, rows, width)).reshape(length, width)


def items_first(array):
    return jnp.transpose(array.reshape(array.shape[0], array.shape[2], array.shape[3]), (1, 0, 2))


def attend_items(pieces):
    q_group, k_group, v_group = pieces
    q_heads = items_first(q_group)
    k_heads = items_first(k_group)
    v_heads = items_first(v_group)
    stacked = jnp.stack([k_heads, v_heads])
    other = partner(stacked, "blk", 0)
    tiles = (q_heads, k_heads, v_heads, other[0], other[1])
    outcome = lax.map(attend_item, tiles)
    count, length, width = outcome.shape
    outcome = jnp.transpose(outcome, (1, 0, 2)).reshape(length, 1, count, width)
    return lax.all_to_all(outcome, "seq", split_axis=0, concat_axis=1, tiled=True)


def on_device(query, keys, values):
    groups = lax.axis_size("seq")
    width = query.shape[1] // HEADS
    tok_rows = query.shape[0]
    key_source, value_source = (keys, values)
    per_dev = (HEADS + groups - 1) // groups
    slots_all = per_dev * groups

    def split_heads(array):
        count_rows = array.shape[0]
        shaped = array.reshape(count_rows, HEADS, width)
        shaped = jnp.pad(shaped, ((0, 0), (0, slots_all - HEADS), (0, 0)))
        return shaped.reshape(count_rows, groups, per_dev, width)

    result = attend_items(
        (
            lax.all_to_all(split_heads(query), "seq", split_axis=1, concat_axis=0, tiled=True),
            lax.all_to_all(split_heads(key_source), "seq", split_axis=1, concat_axis=0, tiled=True),
            lax.all_to_all(
                split_heads(value_source), "seq", split_axis=1, concat_axis=0, tiled=True
            ),
        )
    )
    result = result.reshape(tok_rows, slots_all, width)[:, :HEADS]
    return result.reshape(tok_rows, HEADS * width)


def solution(mesh):
    placed = (P(("blk", "seq"), None), P(("blk", "seq"), None), P(("blk", "seq"), None))
    return jax.shard_map(
        on_device, mesh=mesh, in_specs=placed, out_specs=P(("blk", "seq"), None), check_vma=False
    )
```

profile of v0, /device:TPU:1, one launch (start us, length us, event | category | flops | bytes accessed | tf_op | source)
XLA Modules:
  0.0 233.7 jit_solution(4771804103604966979)
XLA Ops:
  3.1 10.3 %all-to-all-start.1 = ((bf16[64,64,1,128]{3,0,2,1:T(8,128)(2,1)}), bf16[64,64,1,128]{3,0,2,1:T(8,128)(2,1)S(1)}, u32[]{:S(2)}, u32[]{:S(2)}) async-start(bf16[64,64,1,128]{3,0,2,1:T(8,128)(2,1)} %copy.16), calls=%async_computation.1 | async-start | bytes 2097152 | tf_op jit(solution)/shard_map/all_to_all | solution.py:87
  15.5 15.8 %all-to-all-done.1 = bf16[64,64,1,128]{3,0,2,1:T(8,128)(2,1)S(1)} async-done(((bf16[64,64,1,128]{3,0,2,1:T(8,128)(2,1)}), bf16[64,64,1,128]{3,0,2,1:T(8,128)(2,1)S(1)}, u32[]{:S(2)}, u32[]{:S(2)}) %all-to-all-start.1) | async-done | bytes 1048608 | tf_op jit(solution)/shard_map/all_to_all | solution.py:87
  31.3 22.4 %all_to_all.60 = bf16[64,64,1,128]{3,0,2,1:T(8,128)(2,1)S(1)} all-to-all(bf16[64,64,1,128]{3,0,2,1:T(8,128)(2,1)S(1)} %copy.17), channel_id=1, replica_groups=mesh['seq'=64,'blk'=2] {'seq'}, dimensions={1} | all-to-all | bytes 2097152 | tf_op jit(solution)/shard_map/all_to_all | solution.py:88
  53.9 3.4 %collective-permute-start = (bf16[2,1,4096,128]{3,2,1,0:T(8,128)(2,1)S(1)}, bf16[2,1,4096,128]{3,2,1,0:T(8,128)(2,1)}, u32[]{:S(2)}, u32[]{:S(2)}) collective-permute-start(bf16[2,1,4096,128]{3,2,1,0:T(8,128)(2,1)S(1)} %pad_maximum_fusion), channel_id=1, source_target_pairs={{0,1},{1,0},{2,3},{3,2},{4,5},{5,4},{6,7},{7,6},{8,9},{9,8},{10,11... | collective-permute-start | bytes 6291464 | tf_op jit(solution)/shard_map/ppermute | solution.py:12
  60.4 5.4 %all-to-all-start = ((bf16[64,64,1,128]{3,0,2,1:T(8,128)(2,1)}), bf16[64,64,1,128]{3,0,2,1:T(8,128)(2,1)}, u32[]{:S(2)}, u32[]{:S(2)}) async-start(bf16[64,64,1,128]{3,0,2,1:T(8,128)(2,1)} %copy.15), calls=%async_computation | async-start | bytes 2097152 | tf_op jit(solution)/shard_map/all_to_all | solution.py:86
  65.8 47.9 %collective-permute-done = bf16[2,1,4096,128]{3,2,1,0:T(8,128)(2,1)} collective-permute-done((bf16[2,1,4096,128]{3,2,1,0:T(8,128)(2,1)S(1)}, bf16[2,1,4096,128]{3,2,1,0:T(8,128)(2,1)}, u32[]{:S(2)}, u32[]{:S(2)}) %collective-permute-start) | collective-permute-done | bytes 2097184 | tf_op jit(solution)/shard_map/ppermute | solution.py:12
  115.4 90.2 %while.17 = (s32[]{:T(128)}, bf16[8,512,128]{2,1,0:T(8,128)(2,1)}, bf16[8,512,128]{2,1,0:T(8,128)(2,1)}, bf16[4096,128]{1,0:T(8,128)(2,1)S(1)}, bf16[4096,128]{1...) while((s32[]{:T(128)}, bf16[8,512,128]{2,1,0:T(8,128)(2,1)}, ...), condition=%wide.region_5.6_spmd, body=%wide.region_0.5_spmd.sunk | while | flops 2181366784 | bytes 59676272 | solution.py:49
  115.4 2.2 multiply_reduce_fusion.4
  117.6 2.2 multiply_reduce_fusion.5
  119.9 3.1 %fusion.62 = (f32[512]{0:T(512)S(1)}, f32[512]{0:T(512)S(1)}) fusion(f32[512,4096]{1,0:T(8,128)S(1)} %get-tuple-element.143, f32[512]{0:T(512)S(1)} %get-tuple-element.144, f32[512]{0:T(512)S(1)} %get-tuple-element.142, f32[512,4096]{1,0:T(8,128)S(1)} %get-tuple-element.141), kind=kLoop, calls=%fused_computation.4.clone.1 | loop fusion | flops 12581888 | bytes 16785408 | tf_op jit(solution)/shard_map/while/body/eval_jaxpr/while/body/eval_jaxpr/reduce_sum | solution.py:21
  128.9 2.2 multiply_reduce_fusion.5
  131.2 3.1 %fusion.62 = (f32[512]{0:T(512)S(1)}, f32[512]{0:T(512)S(1)}) fusion(f32[512,4096]{1,0:T(8,128)S(1)} %get-tuple-element.143, f32[512]{0:T(512)S(1)} %get-tuple-element.144, f32[512]{0:T(512)S(1)} %get-tuple-element.142, f32[512,4096]{1,0:T(8,128)S(1)} %get-tuple-element.141), kind=kLoop, calls=%fused_computation.4.clone.1 | loop fusion | flops 12581888 | bytes 16785408 | tf_op jit(solution)/shard_map/while/body/eval_jaxpr/while/body/eval_jaxpr/reduce_sum | solution.py:21
  140.2 2.2 multiply_reduce_fusion.5
  142.4 3.1 %fusion.62 = (f32[512]{0:T(512)S(1)}, f32[512]{0:T(512)S(1)}) fusion(f32[512,4096]{1,0:T(8,128)S(1)} %get-tuple-element.143, f32[512]{0:T(512)S(1)} %get-tuple-element.144, f32[512]{0:T(512)S(1)} %get-tuple-element.142, f32[512,4096]{1,0:T(8,128)S(1)} %get-tuple-element.141), kind=kLoop, calls=%fused_computation.4.clone.1 | loop fusion | flops 12581888 | bytes 16785408 | tf_op jit(solution)/shard_map/while/body/eval_jaxpr/while/body/eval_jaxpr/reduce_sum | solution.py:21
  151.5 2.2 multiply_reduce_fusion.5
  153.7 3.1 %fusion.62 = (f32[512]{0:T(512)S(1)}, f32[512]{0:T(512)S(1)}) fusion(f32[512,4096]{1,0:T(8,128)S(1)} %get-tuple-element.143, f32[512]{0:T(512)S(1)} %get-tuple-element.144, f32[512]{0:T(512)S(1)} %get-tuple-element.142, f32[512,4096]{1,0:T(8,128)S(1)} %get-tuple-element.141), kind=kLoop, calls=%fused_computation.4.clone.1 | loop fusion | flops 12581888 | bytes 16785408 | tf_op jit(solution)/shard_map/while/body/eval_jaxpr/while/body/eval_jaxpr/reduce_sum | solution.py:21
  162.7 2.2 multiply_reduce_fusion.5
  165.0 3.1 %fusion.62 = (f32[512]{0:T(512)S(1)}, f32[512]{0:T(512)S(1)}) fusion(f32[512,4096]{1,0:T(8,128)S(1)} %get-tuple-element.143, f32[512]{0:T(512)S(1)} %get-tuple-element.144, f32[512]{0:T(512)S(1)} %get-tuple-element.142, f32[512,4096]{1,0:T(8,128)S(1)} %get-tuple-element.141), kind=kLoop, calls=%fused_computation.4.clone.1 | loop fusion | flops 12581888 | bytes 16785408 | tf_op jit(solution)/shard_map/while/body/eval_jaxpr/while/body/eval_jaxpr/reduce_sum | solution.py:21
  174.0 2.2 multiply_reduce_fusion.5
  176.3 3.1 %fusion.62 = (f32[512]{0:T(512)S(1)}, f32[512]{0:T(512)S(1)}) fusion(f32[512,4096]{1,0:T(8,128)S(1)} %get-tuple-element.143, f32[512]{0:T(512)S(1)} %get-tuple-element.144, f32[512]{0:T(512)S(1)} %get-tuple-element.142, f32[512,4096]{1,0:T(8,128)S(1)} %get-tuple-element.141), kind=kLoop, calls=%fused_computation.4.clone.1 | loop fusion | flops 12581888 | bytes 16785408 | tf_op jit(solution)/shard_map/while/body/eval_jaxpr/while/body/eval_jaxpr/reduce_sum | solution.py:21
  187.5 3.1 %fusion.62 = (f32[512]{0:T(512)S(1)}, f32[512]{0:T(512)S(1)}) fusion(f32[512,4096]{1,0:T(8,128)S(1)} %get-tuple-element.143, f32[512]{0:T(512)S(1)} %get-tuple-element.144, f32[512]{0:T(512)S(1)} %get-tuple-element.142, f32[512,4096]{1,0:T(8,128)S(1)} %get-tuple-element.141), kind=kLoop, calls=%fused_computation.4.clone.1 | loop fusion | flops 12581888 | bytes 16785408 | tf_op jit(solution)/shard_map/while/body/eval_jaxpr/while/body/eval_jaxpr/reduce_sum | solution.py:21
  198.8 3.1 %fusion.62 = (f32[512]{0:T(512)S(1)}, f32[512]{0:T(512)S(1)}) fusion(f32[512,4096]{1,0:T(8,128)S(1)} %get-tuple-element.143, f32[512]{0:T(512)S(1)} %get-tuple-element.144, f32[512]{0:T(512)S(1)} %get-tuple-element.142, f32[512,4096]{1,0:T(8,128)S(1)} %get-tuple-element.141), kind=kLoop, calls=%fused_computation.4.clone.1 | loop fusion | flops 12581888 | bytes 16785408 | tf_op jit(solution)/shard_map/while/body/eval_jaxpr/while/body/eval_jaxpr/reduce_sum | solution.py:21
  206.1 2.7 %reduce = bf16[4096,128]{1,0:T(8,128)(2,1)S(1)} reduce(bf16[4096,1,1,128]{3,0,2,1:T(8,128)(2,1)} %bitcast.20, bf16[]{:T(256)} %broadcast.38), dimensions={1,2}, to_apply=%copy.18.reduce_sub_computation | reduce | bytes 2097154 | tf_op jit(solution)/shard_map/reshape;transpose | solution.py:66
  209.1 22.4 %all_to_all.61 = bf16[64,2,4096]{2,1,0:T(2,128)(2,1)S(1)} all-to-all(bf16[64,2,4096]{2,1,0:T(2,128)(2,1)S(1)} %reshape.79), channel_id=1, replica_groups=mesh['seq'=64,'blk'=2] {'seq'}, dimensions={0} | all-to-all | bytes 2097152 | tf_op jit(solution)/shard_map/all_to_all | solution.py:67
  (69 shorter events, 62.3 us)
Async XLA Ops:
  3.1 28.3 %all-to-all-start.1 = ((bf16[64,64,1,128]{3,0,2,1:T(8,128)(2,1)}), bf16[64,64,1,128]{3,0,2,1:T(8,128)(2,1)S(1)}, u32[]{:S(2)}, u32[]{:S(2)}) async-start(bf16[64,64,1,128]{3,0,2,1:T(8,128)(2,1)} %copy.16), calls=%async_computation.1 | async-start | bytes 2097152 | tf_op jit(solution)/shard_map/all_to_all | solution.py:87
  53.7 4.8 %copy-start = (bf16[64,64,1,128]{3,0,2,1:T(8,128)(2,1)}, bf16[64,64,1,128]{3,0,2,1:T(8,128)(2,1)S(1)}, u32[]{:S(2)}) copy-start(bf16[64,64,1,128]{3,0,2,1:T(8,128)(2,1)S(1)} %all_to_all.60) | copy-start | bytes 3145732
  53.9 59.8 %collective-permute-start = (bf16[2,1,4096,128]{3,2,1,0:T(8,128)(2,1)S(1)}, bf16[2,1,4096,128]{3,2,1,0:T(8,128)(2,1)}, u32[]{:S(2)}, u32[]{:S(2)}) collective-permute-start(bf16[2,1,4096,128]{3,2,1,0:T(8,128)(2,1)S(1)} %pad_maximum_fusion), channel_id=1, source_target_pairs={{0,1},{1,0},{2,3},{3,2},{4,5},{5,4},{6,7},{7,6},{8,9},{9,8},{10,11... | collective-permute-start | bytes 6291464 | tf_op jit(solution)/shard_map/ppermute | solution.py:12
  60.4 55.0 %all-to-all-start = ((bf16[64,64,1,128]{3,0,2,1:T(8,128)(2,1)}), bf16[64,64,1,128]{3,0,2,1:T(8,128)(2,1)}, u32[]{:S(2)}, u32[]{:S(2)}) async-start(bf16[64,64,1,128]{3,0,2,1:T(8,128)(2,1)} %copy.15), calls=%async_computation | async-start | bytes 2097152 | tf_op jit(solution)/shard_map/all_to_all | solution.py:86
  123.0 1.5 copy-start.1
  134.3 1.5 copy-start.1
  145.6 1.5 copy-start.1
  156.8 1.5 copy-start.1
  168.1 1.5 copy-start.1
  179.4 1.5 copy-start.1
  190.7 1.5 copy-start.1
  201.9 1.5 copy-start.1
where the time goes:
time: 235 us; the launch traced here: 234 us
  matrix products  64.9 us (28%)
  waiting for transfers between devices  63.8 us (27%)
  blocking collectives  44.8 us (19%)
  other arithmetic  28 us (12%)
  starting transfers between devices  19.1 us (8%)
  local copies, waits for them, and re-layouts  12.8 us (5%)
    ppermute x1, waiting for transfers between devices, partner(): return lax.ppermute(value, axis, pairs)  47.9 us
    dot_general x16, matrix products, partial_block(): lax.dot_general(q_rows, k_tile, (((1,), (1,)), ((), ())), preferred_eleme...  35.8 us
    dot_general x16, matrix products, partial_block(): jnp.dot(expo.astype(jnp.bfloat16), v_tile, preferred_element_type=jnp.flo...  29.1 us
    reduce_sum x8, other arithmetic, partial_block(): totals = jnp.sum(expo, axis=1)  25 us
    all_to_all x1, blocking collectives, attend_items(): lax.all_to_all(outcome, 'seq', split_axis=0, concat_axis=1, tiled=True)  22.4 us
    all_to_all x1, blocking collectives, on_device(): lax.all_to_all(split_heads(value_source), 'seq', split_axis=1, concat_axi...  22.4 us
    all_to_all x1, waiting for transfers between devices, on_device(): lax.all_to_all(split_heads(key_source), 'seq', split_axis=1, concat_axis=...  15.8 us
    all_to_all x1, starting transfers between devices, on_device(): lax.all_to_all(split_heads(key_source), 'seq', split_axis=1, concat_axis=...  10.3 us
  transfers between devices with their start and end apart: 3, of which 2 were waited for; matrix products, arithmetic and copies ran while one was open for 3% of the time, Pallas kernels for 0%

commit v1 on v0

v1 whole, which is shorter than its diff:
```python
import functools
import math

import jax
import jax.numpy as jnp
from jax import lax
from jax.experimental import pallas as pl
from jax.experimental.pallas import tpu as pltpu
from jax.sharding import PartitionSpec as P

HEADS = 40
WIDTH = 128
BLOCK = 64
CHIPS = 64
HALF = CHIPS * BLOCK
TQ = 512
TK = 1024
SLOTS = TK // 2 // BLOCK
CHUNKS = CHIPS // SLOTS
TILES = HALF // TQ
TO_LOG2 = math.log2(math.e) / math.sqrt(WIDTH)
MESH = pl.DeviceIdType.MESH
NT = (((1,), (1,)), ((), ()))
BF16 = jnp.bfloat16
F32 = jnp.float32


def head_of(chip):
    group = chip // 8
    place = lax.rem(lax.rem(chip, 8) + 24 - 3 * group, 8)
    return place < 5, group * 5 + place


def shifted(chip, step, sign):
    step = lax.rem(step * 27 + 7, 64)
    dx, dy, dz = step // 16, lax.rem(step // 4, 4), lax.rem(step, 4)
    x, y = lax.rem(chip // 8, 4), lax.rem(chip, 4)
    z = chip // 32 * 2 + lax.rem(chip // 4, 2)
    x = lax.rem(x + 4 + sign * dx, 4)
    y = lax.rem(y + 4 + sign * dy, 4)
    z = lax.rem(z + 4 + sign * dz, 4)
    return z // 2 * 32 + x * 8 + lax.rem(z, 2) * 4 + y


def kernel(
    q_in, k_in, v_in, out,
    q_got, k_got, v_got, q_two, v_turned, scores, weights, summed, peak, total, tops, shrink, result,
    q_sent, k_sent, v_sent, o_sent, q_here, k_here, v_here, o_here, passed, fetched,
):
    blk, seq = lax.axis_index("blk"), lax.axis_index("seq")
    core = lax.rem(seq, 2)
    chip = blk * 32 + seq // 2
    owner, head = head_of(chip)

    def device(other):
        return {"blk": other // 32, "seq": lax.rem(other, 32) * 2 + core}

    peer = {"blk": blk, "seq": seq + 1 - 2 * core}

    barrier = pltpu.get_barrier_semaphore()

    @pl.when(owner)
    def _():
        @pl.loop(1, CHIPS)
        def _(i):
            pl.semaphore_signal(barrier, inc=1, device_id=device(lax.rem(chip + i, CHIPS)), device_id_type=MESH)

        pl.semaphore_signal(barrier, inc=1, device_id=peer, device_id_type=MESH)
        pl.semaphore_wait(barrier, HEADS)

    @pl.when(jnp.logical_not(owner))
    def _():
        pl.semaphore_wait(barrier, HEADS)

    def send(src, dst, send_sem, recv_sem, to):
        @pl.when(to != chip)
        def _():
            pltpu.make_async_remote_copy(
                src_ref=src, dst_ref=dst, send_sem=send_sem, recv_sem=recv_sem,
                device_id=device(to), device_id_type=MESH,
            ).start()

        @pl.when(to == chip)
        def _():
            pltpu.make_async_copy(src, dst, recv_sem).start()

    def settle(ref, sem):
        pltpu.make_async_copy(ref, ref, sem).wait()

    @pl.loop(0, CHIPS)
    def _(i):
        to = shifted(chip, i, 1)
        owns, h = head_of(to)

        @pl.when(owns)
        def _():
            cols = pl.ds(pl.multiple_of(h * WIDTH, WIDTH), WIDTH)
            rows = pl.ds(pl.multiple_of(i * BLOCK, BLOCK), BLOCK)
            send(q_in.at[:, cols], q_got.at[rows], q_sent, q_here, to)

    @pl.loop(0, CHIPS)
    def _(i):
        to = shifted(chip, i, 1)
        owns, h = head_of(to)
        c = i // SLOTS

        @pl.when(owns)
        def _():
            cols = pl.ds(pl.multiple_of(h * WIDTH, WIDTH), WIDTH)
            first = c * TK + core * (TK // 2) + lax.rem(i, SLOTS) * BLOCK
            rows = pl.ds(pl.multiple_of(first, BLOCK), BLOCK)
            send(k_in.at[:, cols], k_got.at[rows], k_sent, k_here.at[c], to)
            send(v_in.at[:, cols], v_got.at[rows], v_sent, v_here.at[c], to)

    def mine(c):
        return pl.ds(pl.multiple_of(c * TK + core * (TK // 2), TK // 2), TK // 2)

    def theirs(c):
        return pl.ds(pl.multiple_of(c * TK + (1 - core) * (TK // 2), TK // 2), TK // 2)

    def passing(ref, c, which):
        return pltpu.make_async_remote_copy(
            src_ref=ref.at[mine(c)], dst_ref=ref.at[mine(c)], send_sem=passed.at[which, c],
            recv_sem=fetched.at[which, c], device_id=peer, device_id_type=MESH,
        )

    def pass_on(c):
        settle(k_got.at[mine(c)], k_here.at[c])
        passing(k_got, c, 0).start()
        settle(v_got.at[mine(c)], v_here.at[c])
        passing(v_got, c, 1).start()

    def take(c):
        settle(k_got.at[theirs(c)], fetched.at[0, c])
        settle(v_got.at[theirs(c)], fetched.at[1, c])

    def chunk(c):
        return pl.ds(pl.multiple_of(c * TK, TK), TK)

    def prepare():
        settle(q_got, q_here)

        @pl.loop(0, HALF // 256)
        def _(i):
            rows = pl.ds(pl.multiple_of(i * 256, 256), 256)
            scaled = q_got[rows, :].astype(F32) * TO_LOG2
            high = scaled.astype(BF16)
            q_two[rows, 0:WIDTH] = high
            q_two[rows, WIDTH : 2 * WIDTH] = (scaled - high.astype(F32)).astype(BF16)

        peak[...] = jnp.full(peak.shape, -jnp.inf, F32)
        total[...] = jnp.zeros(total.shape, F32)
        summed[...] = jnp.zeros(summed.shape, F32)
        shrink[...] = jnp.ones(shrink.shape, F32)
        weights[...] = jnp.zeros(weights.shape, BF16)
        scores[1] = jnp.full(scores.shape[1:], -1e30, F32)
        tops[...] = jnp.full(tops.shape, -1e30, F32)

    def turn(c):
        for x in range(TK // 512):
            rows = pl.ds(pl.multiple_of(c * TK + x * 512, 512), 512)
            v_turned[:, rows] = v_got[rows, :].T

    def score(c, i, slot):
        keys = k_got[chunk(c), :]
        s = lax.dot_general(
            jnp.concatenate([keys, keys], axis=1), q_two[i * TQ : (i + 1) * TQ, :], NT,
            preferred_element_type=F32,
        )
        scores[slot] = s
        tops[slot] = jnp.max(s, axis=0, keepdims=True)

    def weigh(i, slot):
        old = peak[i]
        new = jnp.maximum(old, tops[slot])
        factor = jnp.exp2(old - new)
        w = jnp.exp2(scores[slot] - new)
        total[i] = total[i] * factor + jnp.sum(w, axis=0, keepdims=True)
        weights[slot] = w.astype(BF16)
        peak[i] = new
        shrink[slot] = factor

    def gather(c, i, slot):
        got = jnp.dot(v_turned[:, chunk(c)], weights[slot], preferred_element_type=F32)
        summed[i] = summed[i] * shrink[slot] + got

    def finish(i):
        result[i * TQ : (i + 1) * TQ, :] = (summed[i] / total[i]).T.astype(BF16)

    def send_back(i):
        cols = pl.ds(pl.multiple_of(head * WIDTH, WIDTH), WIDTH)

        @pl.loop(i * (TQ // BLOCK), (i + 1) * (TQ // BLOCK))
        def _(s):
            rows = pl.ds(pl.multiple_of(s * BLOCK, BLOCK), BLOCK)
            send(result.at[rows], out.at[:, cols], o_sent, o_here, shifted(chip, s, -1))

    last = TILES - 1

    def over_chunk(c, final):
        before = jnp.maximum(c - 1, 0)
        take(c)
        turn(c)
        score(c, 0, 0)
        weigh(last, 1)
        gather(before, last - 1, 0)
        for i in range(last):
            if i == TILES // 2 and not final:
                pass_on(c + 1)
            score(c, i + 1, (i + 1) % 2)
            weigh(i, i % 2)
            if i == 0:
                gather(before, last, 1)
            else:
                gather(c, i - 1, (i - 1) % 2)
                if final:
                    finish(i - 1)
                    if i >= 2:
                        send_back(i - 2)

    @pl.when(owner)
    def _():
        prepare()
        pass_on(0)

        @pl.loop(0, CHUNKS - 1)
        def _(c):
            over_chunk(c, False)

        over_chunk(CHUNKS - 1, True)
        weigh(last, 1)
        gather(CHUNKS - 1, last - 1, 0)
        finish(last - 1)
        send_back(last - 2)
        gather(CHUNKS - 1, last, 1)
        finish(last)
        send_back(last - 1)
        send_back(last)
        for c in range(CHUNKS):
            passing(k_got, c, 0).wait_send()
            passing(v_got, c, 1).wait_send()

        mine_too = result.at[pl.ds(0, (CHIPS - 1) * BLOCK)]
        settle(mine_too, o_sent)
        less = pl.ds(0, (HEADS - 1) * WIDTH)
        settle(q_in.at[:, less], q_sent)
        settle(k_in.at[:, less], k_sent)
        settle(v_in.at[:, less], v_sent)

    @pl.when(jnp.logical_not(owner))
    def _():
        settle(q_in, q_sent)
        settle(k_in, k_sent)
        settle(v_in, v_sent)

    settle(out, o_here)


def on_device(query, keys, values):
    dma = pltpu.SemaphoreType.DMA
    return pl.pallas_call(
        kernel,
        out_shape=jax.ShapeDtypeStruct(query.shape, query.dtype),
        in_specs=[pl.BlockSpec(memory_space=pl.ANY)] * 3,
        out_specs=pl.BlockSpec(memory_space=pl.ANY),
        scratch_shapes=[
            pltpu.VMEM((HALF, WIDTH), BF16),
            pltpu.VMEM((2 * HALF, WIDTH), BF16),
            pltpu.VMEM((2 * HALF, WIDTH), BF16),
            pltpu.VMEM((HALF, 2 * WIDTH), BF16),
            pltpu.VMEM((WIDTH, 2 * HALF), BF16),
            pltpu.VMEM((2, TK, TQ), F32),
            pltpu.VMEM((2, TK, TQ), BF16),
            pltpu.VMEM((TILES, WIDTH, TQ), F32),
            pltpu.VMEM((TILES, 1, TQ), F32),
            pltpu.VMEM((TILES, 1, TQ), F32),
            pltpu.VMEM((2, 1, TQ), F32),
            pltpu.VMEM((2, 1, TQ), F32),
            pltpu.VMEM((HALF, WIDTH), BF16),
            dma, dma, dma, dma, dma,
            dma((CHUNKS,)), dma((CHUNKS,)), dma, dma((2, CHUNKS)), dma((2, CHUNKS)),
        ],
        compiler_params=pltpu.CompilerParams(
            collective_id=0, has_side_effects=True, vmem_limit_bytes=60 * 2**20
        ),
    )(query, keys, values)


def solution(mesh):
    placed = P(("blk", "seq"), None)
    return jax.shard_map(
        on_device, mesh=mesh, in_specs=(placed,) * 3, out_specs=placed, check_vma=False
    )
```

time: 235 us -> 109 us (0.46)
  the two profiles are of different devices: /device:TPU:1 before, /device:TPU:9 now
where the time goes in v1:
time: 109 us
  Pallas kernels  107 us (98%)
  local copies, waits for them, and re-layouts  1.97 us (2%)
    pallas_call x1, Pallas kernels, on_device(): pl.pallas_call(kernel, out_shape=jax.ShapeDtypeStruct(query.shape, query....  107 us

profile of v1, /device:TPU:9, one launch (start us, length us, event | category | flops | bytes accessed | tf_op | source)
XLA Modules:
  0.0 109.0 jit_solution(4531860961103073803)
XLA Ops:
  0.0 107.0 %shard_map.37 = bf16[64,5120]{1,0:T(8,128)(2,1)} custom-call(bf16[64,5120]{1,0:T(8,128)(2,1)} %q_in.1, bf16[64,5120]{1,0:T(8,128)(2,1)} %k_in.1, bf16[64,5120]{1,0:T(8,128)(2,1)} %v_in.1), custom_call_target="tpu_custom_call" | custom-call | tf_op jit(solution)/shard_map/pallas_call | solution.py:261
  107.0 2.0 %copy.5 = bf16[64,5120]{1,0:T(8,128)(2,1)} copy(bf16[64,5120]{1,0:T(8,128)(2,1)} %shard_map.37) | data formatting | bytes 1310720

commit v2 on v1

v2 whole, which is shorter than its diff:
```python
import functools
import math

import jax
import jax.numpy as jnp
from jax import lax
from jax.experimental import pallas as pl
from jax.experimental.pallas import tpu as pltpu
from jax.sharding import PartitionSpec as P

HEADS = 40
WIDTH = 128
TALL = WIDTH + 16
BLOCK = 64
CHIPS = 64
HALF = CHIPS * BLOCK
TQ = 512
TK = 1024
GROUPS = 8
OWNERS = HEADS // GROUPS
CHUNKS = GROUPS
STREAMED = 4
TILES = HALF // TQ
TO_LOG2 = math.log2(math.e) / math.sqrt(WIDTH)
MESH = pl.DeviceIdType.MESH
NT = (((1,), (1,)), ((), ()))
BF16 = jnp.bfloat16
F32 = jnp.float32


def owner_place(group, r):
    return lax.rem(r + 3 * group, 8)


def away(c, p):
    return 0 if isinstance(c, int) and c == 0 else lax.rem(p + c + (GROUPS - 2), GROUPS - 1) + 1


def kernel(
    q_in, k_in, v_in, out,
    q_got, k_got, v_got, q_two, v_turned, scores, weights, summed, peak, tops, shrink, result,
    q_sent, k_sent, v_sent, o_sent, q_here, k_here, v_here, o_here, passed, fetched, paced,
):
    blk, seq = lax.axis_index("blk"), lax.axis_index("seq")
    core = lax.rem(seq, 2)
    group, place = blk * 4 + seq // 16, lax.rem(seq // 2, 8)
    mine_r = lax.rem(place + 24 - 3 * group, 8)
    owner = mine_r < 5
    head = group * OWNERS + mine_r
    follower = owner_place(group, mine_r + OWNERS)

    def device(g, p):
        return {"blk": g // 4, "seq": lax.rem(g, 4) * 16 + p * 2 + core}

    peer = {"blk": blk, "seq": seq + 1 - 2 * core}

    barrier = pltpu.get_barrier_semaphore()

    @pl.when(owner)
    def _():
        @pl.loop(0, GROUPS)
        def _(g):
            for p in range(GROUPS):

                @pl.when(jnp.logical_or(g != group, p != place))
                def _():
                    pl.semaphore_signal(barrier, inc=1, device_id=device(g, p), device_id_type=MESH)

        pl.semaphore_signal(barrier, inc=1, device_id=peer, device_id_type=MESH)
        peak[...] = jnp.full(peak.shape, -jnp.inf, F32)
        v_turned[WIDTH:TALL, :] = jnp.ones((TALL - WIDTH, v_turned.shape[1]), BF16)
        summed[...] = jnp.zeros(summed.shape, F32)
        shrink[...] = jnp.ones(shrink.shape, F32)
        weights[...] = jnp.zeros(weights.shape, BF16)
        scores[1] = jnp.full(scores.shape[1:], -1e30, F32)
        tops[...] = jnp.full(tops.shape, -1e30, F32)

    pl.semaphore_wait(barrier, HEADS)

    def settle(ref, sem):
        pltpu.make_async_copy(ref, ref, sem).wait()

    def remote(src, dst, send_sem, recv_sem, g, p):
        pltpu.make_async_remote_copy(
            src_ref=src, dst_ref=dst, send_sem=send_sem, recv_sem=recv_sem,
            device_id=device(g, p), device_id_type=MESH,
        ).start()

    def send(src, dst, send_sem, recv_sem, g, p, near):
        if not near:
            remote(src, dst, send_sem, recv_sem, g, p)
            return

        @pl.when(p != place)
        def _():
            remote(src, dst, send_sem, recv_sem, g, p)

        @pl.when(p == place)
        def _():
            pltpu.make_async_copy(src, dst, recv_sem).start()

    def columns(h):
        return pl.ds(pl.multiple_of(h * WIDTH, WIDTH), WIDTH)

    def targets(c):
        g = lax.rem(group + away(c, place), GROUPS)
        for j in range(OWNERS):
            r = lax.rem(j + place, OWNERS)
            yield g, owner_place(g, r), columns(g * OWNERS + r)

    def send_queries(c, near):
        rows = pl.ds(pl.multiple_of(c * TQ + place * BLOCK, BLOCK), BLOCK)
        for g, p, cols in targets(c):
            send(q_in.at[:, cols], q_got.at[rows], q_sent, q_here, g, p, near)

    def send_keys(c, near):
        rows = pl.ds(pl.multiple_of(c * TK + core * (TK // 2) + place * BLOCK, BLOCK), BLOCK)
        for g, p, cols in targets(c):
            send(k_in.at[:, cols], k_got.at[rows], k_sent.at[c], k_here.at[c], g, p, near)
            send(v_in.at[:, cols], v_got.at[rows], v_sent.at[c], v_here.at[c], g, p, near)

    def some(ref, blocks):
        return ref.at[:, pl.ds(0, blocks * WIDTH)]

    def keys_left(c, blocks):
        settle(some(k_in, blocks), k_sent.at[c])
        settle(some(v_in, blocks), v_sent.at[c])

    send_queries(0, True)

    @pl.loop(1, GROUPS)
    def _(c):
        send_queries(c, False)

    send_keys(0, True)

    def mine(c):
        return pl.ds(pl.multiple_of(c * TK + core * (TK // 2), TK // 2), TK // 2)

    def theirs(c):
        return pl.ds(pl.multiple_of(c * TK + (1 - core) * (TK // 2), TK // 2), TK // 2)

    def passing(ref, c, which):
        return pltpu.make_async_remote_copy(
            src_ref=ref.at[mine(c)], dst_ref=ref.at[mine(c)], send_sem=passed.at[which, c],
            recv_sem=fetched.at[which, c], device_id=peer, device_id_type=MESH,
        )

    def pass_on(c):
        settle(k_got.at[mine(c)], k_here.at[c])
        passing(k_got, c, 0).start()
        settle(v_got.at[mine(c)], v_here.at[c])
        passing(v_got, c, 1).start()

    def take(c):
        settle(k_got.at[theirs(c)], fetched.at[0, c])
        settle(v_got.at[theirs(c)], fetched.at[1, c])

    def chunk(c):
        return pl.ds(pl.multiple_of(c * TK, TK), TK)

    def prepare():
        settle(q_got, q_here)

        @pl.loop(0, HALF // 256)
        def _(i):
            rows = pl.ds(pl.multiple_of(i * 256, 256), 256)
            scaled = q_got[rows, :].astype(F32) * TO_LOG2
            high = scaled.astype(BF16)
            q_two[rows, 0:WIDTH] = high
            q_two[rows, WIDTH : 2 * WIDTH] = (scaled - high.astype(F32)).astype(BF16)

    def turn(c):
        for x in range(TK // 512):
            rows = pl.ds(pl.multiple_of(c * TK + x * 512, 512), 512)
            v_turned[0:WIDTH, rows] = v_got[rows, :].T

    def tile(i):
        return pl.ds(i * TQ if isinstance(i, int) else pl.multiple_of(i * TQ, TQ), TQ)

    def score(c, i, slot):
        keys = k_got[chunk(c), :]
        s = lax.dot_general(
            jnp.concatenate([keys, keys], axis=1), q_two[tile(i), :], NT,
            preferred_element_type=F32,
        )
        scores[slot] = s
        tops[slot] = jnp.max(s, axis=0, keepdims=True)

    def weigh(i, slot):
        old = peak[i]
        new = jnp.maximum(old, tops[slot])
        factor = jnp.exp2(old - new)
        w = jnp.exp2(scores[slot] - new)
        weights[slot] = w.astype(BF16)
        peak[i] = new
        shrink[slot] = factor

    def gather(c, i, slot):
        got = jnp.dot(v_turned[:, chunk(c)], weights[slot], preferred_element_type=F32)
        summed[i] = summed[i] * shrink[slot] + got

    def finish(i):
        result[tile(i), :] = (summed[i, 0:WIDTH, :] / summed[i, WIDTH : WIDTH + 1, :]).T.astype(BF16)

    def send_back(i, near):
        cols = columns(head)
        for p in range(GROUPS):
            g = group if near else lax.rem(group + GROUPS - 1 - lax.rem(i + (p + GROUPS - 2), GROUPS - 1), GROUPS)
            rows = pl.ds(pl.multiple_of(i * TQ + p * BLOCK, BLOCK), BLOCK)
            send(result.at[rows], out.at[:, cols], o_sent, o_here, g, p, near)

    last = TILES - 1

    def over_chunk(c):
        before = jnp.maximum(c - 1, 0)

        @pl.when(c < STREAMED - 1)
        def _():
            @pl.when(mine_r < GROUPS - OWNERS)
            def _():
                pl.semaphore_signal(paced, inc=1, device_id=device(group, follower), device_id_type=MESH)

            send_keys(2 * c + 2, False)
            send_keys(2 * c + 3, False)

        take(c)
        turn(c)
        score(c, 0, 0)
        weigh(last, 1)
        gather(before, last - 1, 0)
        for i in range(last):
            if i == 2:

                @pl.when(c > 0)
                def _():
                    pass_on(2 * c)

            if i == 6:
                pass_on(2 * c + 1)

            score(c, i + 1, (i + 1) % 2)
            weigh(i, i % 2)
            if i == 0:
                gather(before, last, 1)
            else:
                gather(c, i - 1, (i - 1) % 2)

    def over_tile(i):
        first = i == 0
        score(STREAMED, i, 0)
        weigh(jnp.where(first, last, i - 1), 1)
        gather(jnp.where(first, STREAMED - 1, CHUNKS - 2), jnp.where(first, last - 1, i - 1), 0)
        score(STREAMED + 1, i, 1)
        weigh(i, 0)
        before = jnp.where(first, last, i - 1)
        gather(jnp.where(first, STREAMED - 1, CHUNKS - 1), before, 1)
        finish(before)
        score(STREAMED + 2, i, 0)
        weigh(i, 1)
        gather(STREAMED, i, 0)
        score(STREAMED + 3, i, 1)
        weigh(i, 0)
        gather(STREAMED + 1, i, 1)

        @pl.when(i == 1)
        def _():
            send_back(0, True)

        @pl.when(i > 1)
        def _():
            send_back(i - 1, False)

    @pl.when(owner)
    def _():
        settle(some(q_in, HEADS - 1), q_sent)
        send_keys(1, False)
        prepare()
        pass_on(0)

        @pl.loop(0, STREAMED)
        def _(c):
            over_chunk(c)

        for c in range(STREAMED, CHUNKS):
            take(c)
            turn(c)

        @pl.loop(0, TILES)
        def _(i):
            over_tile(i)

        weigh(last, 1)
        gather(CHUNKS - 2, last, 0)
        gather(CHUNKS - 1, last, 1)
        finish(last)
        send_back(last, False)
        for c in range(CHUNKS):
            passing(k_got, c, 0).wait_send()
            passing(v_got, c, 1).wait_send()
            keys_left(c, OWNERS - 1 if c == 0 else OWNERS)
        settle(result.at[pl.ds(0, (CHIPS - 1) * BLOCK)], o_sent)

    @pl.when(jnp.logical_not(owner))
    def _():
        settle(q_in, q_sent)
        send_keys(1, False)

        @pl.loop(0, STREAMED - 1)
        def _(c):
            pl.semaphore_wait(paced, 1)
            send_keys(2 * c + 2, False)
            send_keys(2 * c + 3, False)

        for c in range(CHUNKS):
            keys_left(c, OWNERS)

    settle(out, o_here)


def on_device(query, keys, values):
    dma = pltpu.SemaphoreType.DMA
    return pl.pallas_call(
        kernel,
        out_shape=jax.ShapeDtypeStruct(query.shape, query.dtype),
        in_specs=[pl.BlockSpec(memory_space=pl.ANY)] * 3,
        out_specs=pl.BlockSpec(memory_space=pl.ANY),
        scratch_shapes=[
            pltpu.VMEM((HALF, WIDTH), BF16),
            pltpu.VMEM((2 * HALF, WIDTH), BF16),
            pltpu.VMEM((2 * HALF, WIDTH), BF16),
            pltpu.VMEM((HALF, 2 * WIDTH), BF16),
            pltpu.VMEM((TALL, 2 * HALF), BF16),
            pltpu.VMEM((2, TK, TQ), F32),
            pltpu.VMEM((2, TK, TQ), BF16),
            pltpu.VMEM((TILES, TALL, TQ), F32),
            pltpu.VMEM((TILES, 1, TQ), F32),
            pltpu.VMEM((2, 1, TQ), F32),
            pltpu.VMEM((2, 1, TQ), F32),
            pltpu.VMEM((HALF, WIDTH), BF16),
            dma, dma((CHUNKS,)), dma((CHUNKS,)), dma, dma,
            dma((CHUNKS,)), dma((CHUNKS,)), dma, dma((2, CHUNKS)), dma((2, CHUNKS)), pltpu.SemaphoreType.REGULAR,
        ],
        compiler_params=pltpu.CompilerParams(
            collective_id=0, has_side_effects=True, vmem_limit_bytes=60 * 2**20
        ),
    )(query, keys, values)


def solution(mesh):
    placed = P(("blk", "seq"), None)
    return jax.shard_map(
        on_device, mesh=mesh, in_specs=(placed,) * 3, out_specs=placed, check_vma=False
    )
```

time: 109 us -> 90.6 us (0.83)
  the two profiles are of different devices: /device:TPU:9 before, /device:TPU:1 now
where the time goes in v2:
time: 90.6 us; the launch traced here: 90.5 us
  Pallas kernels  88.5 us (98%)
  local copies, waits for them, and re-layouts  1.97 us (2%)
    pallas_call x1, Pallas kernels, on_device(): pl.pallas_call(kernel, out_shape=jax.ShapeDtypeStruct(query.shape, query....  88.5 us
    unnamed x1, local copies, waits for them, and re-layouts  1.97 us

profile of v2, /device:TPU:1, one launch (start us, length us, event | category | flops | bytes accessed | tf_op | source)
XLA Modules:
  0.0 90.5 jit_solution(4481399258429385920)
XLA Ops:
  0.0 88.5 %shard_map.37 = bf16[64,5120]{1,0:T(8,128)(2,1)} custom-call(bf16[64,5120]{1,0:T(8,128)(2,1)} %q_in.1, bf16[64,5120]{1,0:T(8,128)(2,1)} %k_in.1, bf16[64,5120]{1,0:T(8,128)(2,1)} %v_in.1), custom_call_target="tpu_custom_call" | custom-call | tf_op jit(solution)/shard_map/pallas_call | solution.py:323
  88.5 2.0 %copy.5 = bf16[64,5120]{1,0:T(8,128)(2,1)} copy(bf16[64,5120]{1,0:T(8,128)(2,1)} %shard_map.37) | data formatting | bytes 1310720
